TPU v7x, 768 devices: a whole 4x8x12 slice. The times are simulated.
768 devices in a mesh: gx: 12 (over z), gy: 8 (over y_lo, x), gz: 8 (over y_hi, core).
Axes of the slice: x: 4, y: 8 (y_hi: 4, y_lo: 2; y = y_hi * 2 + y_lo), z: 12, core: 2. Of those that a mesh axis runs over, the one named last changes fastest.
Arguments:
- metric: float32 [6, 192, 128, 1024], P(None, 'gx', 'gy', 'gz'), may hold values from -1 to 9
- curvature: float32 [6, 192, 128, 1024], P(None, 'gx', 'gy', 'gz'), may hold values from -1.8 to 1.8
- conserved: float32 [4, 192, 128, 1024], P(None, 'gx', 'gy', 'gz'), may hold values from -0.3 to 1, as said below
- matter_mask: int32 [12, 8, 64], P('gx', 'gy', 'gz'), may hold values from 0 to 1, as said below
Outputs:
- metric_next: float32 [6, 192, 128, 1024], P(None, 'gx', 'gy', 'gz')
- curvature_next: float32 [6, 192, 128, 1024], P(None, 'gx', 'gy', 'gz')
- conserved_next: float32 [4, 192, 128, 1024], P(None, 'gx', 'gy', 'gz')
Inputs may be any that keep to these rules, and one draw needn't show every extreme that they name: `conserved`: component 0 is the density, from 0.25 to 1; components 1 to 3 are the momentum. `matter_mask`: 1 marks a matter-bearing meshblock of 16 x 16 x 16 cells.
All inputs are finite; a program needn't handle non-finite values.
Results may differ from a plain program's by a relative error of at most 0.00002.
Values sent between devices are 32-bit elements; how exact they have to be, the bound alone decides.
A program may use at most 32 MiB of HBM per device.

v0:
```python
import math

import jax
import jax.numpy as jnp
from jax import lax
from jax.sharding import Mesh
from jax.sharding import PartitionSpec as P

MB = 16
GX_GY_GZ = ("gx", "gy_0", "gy_1", "gz_0", "gz_1")
GY = ("gy_0", "gy_1")
GZ = ("gz_0", "gz_1")


second_stencil = (1.0 / 90.0, -3.0 / 20.0, 1.5, -49.0 / 18.0, 1.5, -3.0 / 20.0, 1.0 / 90.0)
first_stencil = (-1.0 / 60.0, 3.0 / 20.0, -0.75, 0.0, 0.75, -3.0 / 20.0, 1.0 / 60.0)
sound_square = 0.25
sound_speed = 0.5
courant = 0.3
eight_pi = 8.0 * math.pi
pair_first = (0, 0, 0, 1, 1, 2)
pair_second = (0, 1, 2, 1, 2, 2)


def over_axes(value, axes):
    for axis in axes:
        value = lax.pmax(value, axis)
    return value


def padded_2(value, sides, width):
    edges = {}
    for axis, dim in sides:
        peers, length = (lax.axis_size(axis), value.shape[dim])
        up = [(i, (i + 1) % peers) for i in range(peers)]
        last = lax.slice_in_dim(value, length - width, length, axis=dim)
        first = lax.slice_in_dim(value, 0, width, axis=dim)
        edges[dim] = (
            lax.ppermute(last, axis, up),
            lax.ppermute(first, axis, [(b, a) for a, b in up]),
        )
    done = []
    for _, dim in sides:
        low, high = edges[dim]
        around = [(width, width) if d in done else (0, 0) for d in range(value.ndim)]
        value = jnp.concatenate([jnp.pad(low, around), value, jnp.pad(high, around)], axis=dim)
        done.append(dim)
    return value


def expand_mask(matter_mask, block_edge):
    blocks_x, blocks_y, blocks_z = matter_mask.shape
    spread = jnp.broadcast_to(
        matter_mask[:, None, :, None, :, None],
        (blocks_x, block_edge, blocks_y, block_edge, blocks_z, block_edge),
    )
    return spread.reshape(blocks_x * block_edge, blocks_y * block_edge, blocks_z * block_edge) > 0


def shifted(padded, margin, extent, direction, offset):
    starts = [margin, margin, margin]
    starts[direction] = starts[direction] + offset
    return padded[
        :,
        starts[0] : starts[0] + extent[0],
        starts[1] : starts[1] + extent[1],
        starts[2] : starts[2] + extent[2],
    ]


def strip_along(padded, margin, extent, direction):
    starts = [margin, margin, margin]
    stops = [margin + extent[0], margin + extent[1], margin + extent[2]]
    starts[direction] = starts[direction] - 1
    stops[direction] = stops[direction] + 1
    return padded[:, starts[0] : stops[0], starts[1] : stops[1], starts[2] : stops[2]]


def stencil_sum(padded, margin, extent, stencil, direction):
    total = jnp.zeros((padded.shape[0],) + tuple(extent), jnp.float32)
    for offset in range(-3, 4):
        if stencil[offset + 3] != 0.0:
            total = total + stencil[offset + 3] * shifted(padded, margin, extent, direction, offset)
    return total


def advance_fluid(fluid_padded, potential_padded, extent, speed_max, step):
    center = shifted(fluid_padded, 1, extent, 0, 0)
    density = center[0]
    divergence = jnp.zeros_like(center)
    for direction in range(3):
        strip = strip_along(fluid_padded, 1, extent, direction)
        strip_density = strip[0]
        strip_moment = strip[1:4]
        velocity = strip_moment[direction] / strip_density
        flux_moment = strip_moment * velocity[None]
        flux_moment = flux_moment.at[direction].add(sound_square * strip_density)
        flux = jnp.concatenate([strip_moment[direction][None], flux_moment], axis=0)
        length = strip.shape[direction + 1]
        lower_flux = lax.slice_in_dim(flux, 0, length - 1, axis=direction + 1)
        upper_flux = lax.slice_in_dim(flux, 1, length, axis=direction + 1)
        lower_state = lax.slice_in_dim(strip, 0, length - 1, axis=direction + 1)
        upper_state = lax.slice_in_dim(strip, 1, length, axis=direction + 1)
        face = 0.5 * (lower_flux + upper_flux) - 0.5 * speed_max * (upper_state - lower_state)
        faces = length - 1
        divergence = divergence + (
            lax.slice_in_dim(face, 1, faces, axis=direction + 1)
            - lax.slice_in_dim(face, 0, faces - 1, axis=direction + 1)
        )
    gradient = jnp.concatenate(
        [
            stencil_sum(potential_padded, 3, extent, first_stencil, direction)
            for direction in range(3)
        ],
        axis=0,
    )
    source = jnp.concatenate([jnp.zeros_like(density)[None], density[None] * gradient], axis=0)
    return center - step * divergence + step * source


def body(metric, curvature, conserved, matter_mask):
    extent = (metric.shape[1], metric.shape[2], metric.shape[3])
    cell_mask = expand_mask(matter_mask, MB)
    density = conserved[0]
    moment = conserved[1:4]
    speed = jnp.max(jnp.abs(moment), axis=0) / density + sound_speed
    local_speed = jnp.max(jnp.where(cell_mask, speed, jnp.float32(sound_speed)))
    speed_max = over_axes(local_speed, GX_GY_GZ)
    step = courant / speed_max
    stacked = jnp.concatenate([metric, conserved], axis=0)
    padded_all = padded_2(stacked, (("gx", 1), (GY, 2), (GZ, 3)), 3)
    metric_padded = padded_all[:6]
    fluid_padded = padded_all[6:, 2:-2, 2:-2, 2:-2]
    laplacian = stencil_sum(metric_padded, 3, extent, second_stencil, 0)
    laplacian = laplacian + stencil_sum(metric_padded, 3, extent, second_stencil, 1)
    laplacian = laplacian + stencil_sum(metric_padded, 3, extent, second_stencil, 2)
    stress_list = []
    for component in range(6):
        first = pair_first[component]
        second = pair_second[component]
        term = moment[first] * moment[second] / density
        if first == second:
            term = term + sound_square * density
        stress_list.append(term)
    stress = jnp.stack(stress_list)
    curvature_next = curvature + step * (eight_pi * stress - 0.5 * laplacian)
    metric_next = metric - 2.0 * step * curvature
    potential_padded = 0.5 * (metric_padded[0:1] + metric_padded[3:4] + metric_padded[5:6])
    advanced = advance_fluid(fluid_padded, potential_padded, extent, speed_max, step)
    conserved_next = jnp.where(cell_mask[None], advanced, conserved)
    return (metric_next, curvature_next, conserved_next)


def solution(mesh):
    split = Mesh(
        mesh.devices.reshape(mesh.shape["gx"], 2, 4, 4, 2), ("gx", "gy_0", "gy_1", "gz_0", "gz_1")
    )
    placed = (P(None, "gx", GY, GZ), P(None, "gx", GY, GZ), P(None, "gx", GY, GZ), P("gx", GY, GZ))
    return jax.shard_map(
        body,
        mesh=split,
        in_specs=placed,
        out_specs=(P(None, "gx", GY, GZ), P(None, "gx", GY, GZ), P(None, "gx", GY, GZ)),
        check_vma=False,
    )
```

profile of v0, /device:TPU:1, one launch (start us, length us, event | category | flops | bytes accessed | tf_op | source)
XLA Modules:
  0.0 129.0 jit_solution(11212362032461585383)
XLA Ops:
  0.6 1.1 abs_reduce_fusion
  2.6 1.6 %select_reduce_fusion = f32[]{:T(128)} fusion(f32[16,16,128]{2,1,0:T(8,128)S(1)} %abs_reduce_fusion, pred[128]{0:T(512)(128)(4,1)S(1)} %broadcast_in_dim.25, f32[4,16,16,128]{3,2,1,0:T(8,128)} %param.12), kind=kLoop, calls=%fused_computation.178 | loop fusion | flops 131071 | bytes 262276 | tf_op jit(solution)/shard_map/reduce_max | solution.py:127
  4.1 29.2 %pmax.35 = f32[]{:T(128)} all-reduce(f32[]{:T(128)} %select_reduce_fusion), channel_id=1, replica_groups=mesh['gx'=12,'gy_0'=2,'gy_1'=4,'gz_0'=4,'gz_1'=2] {'gx'}, use_global_device_ids=true, to_apply=%region_2.3 | all-reduce | flops 1 | bytes 8 | tf_op jit(solution)/shard_map/pmax | solution.py:27
  33.3 4.4 %pmax.36 = f32[]{:T(128)} all-reduce(f32[]{:T(128)} %pmax.35), channel_id=1, replica_groups=mesh['gx'=12,'gy_0'=2,'gy_1'=4,'gz_0'=4,'gz_1'=2] {'gy_0'}, use_global_device_ids=true, to_apply=%region_3.4 | all-reduce | flops 1 | bytes 8 | tf_op jit(solution)/shard_map/pmax | solution.py:27
  37.7 9.1 %pmax.37 = f32[]{:T(128)} all-reduce(f32[]{:T(128)} %pmax.36), channel_id=1, replica_groups=mesh['gx'=12,'gy_0'=2,'gy_1'=4,'gz_0'=4,'gz_1'=2] {'gy_1'}, use_global_device_ids=true, to_apply=%region_4.5 | all-reduce | flops 1 | bytes 8 | tf_op jit(solution)/shard_map/pmax | solution.py:27
  46.8 11.5 %pmax.38 = f32[]{:T(128)} all-reduce(f32[]{:T(128)} %pmax.37), channel_id=1, replica_groups=mesh['gx'=12,'gy_0'=2,'gy_1'=4,'gz_0'=4,'gz_1'=2] {'gz_0'}, use_global_device_ids=true, to_apply=%region_5.6 | all-reduce | flops 1 | bytes 8 | tf_op jit(solution)/shard_map/pmax | solution.py:27
  58.3 14.2 %pmax.39 = f32[]{:T(128)} all-reduce(f32[]{:T(128)} %pmax.38), channel_id=1, replica_groups=mesh['gx'=12,'gy_0'=2,'gy_1'=4,'gz_0'=4,'gz_1'=2] {'gz_1'}, use_global_device_ids=true, to_apply=%region_6.7 | all-reduce | flops 1 | bytes 8 | tf_op jit(solution)/shard_map/pmax | solution.py:27
  73.2 2.4 %constant_dynamic-update-slice_fusion.1 = (f32[10,16,16,128]{3,2,1,0:T(8,128)S(1)}, f32[6,16,16,128]{3,2,1,0:T(8,128)}) fusion(f32[6,16,16,128]{3,2,1,0:T(8,128)} %param.10, f32[6,16,16,128]{3,2,1,0:T(8,128)} %param.11, f32[]{:T(128)S(6)} %mul_shard_map.3), kind=kLoop, calls=%fused_computation.181 | loop fusion | flops 393215 | bytes 3145732
  76.4 1.9 %collective-permute-start.1 = (f32[10,3,16,128]{3,2,1,0:T(8,128)}, f32[10,3,16,128]{3,2,1,0:T(8,128)S(1)}, u32[]{:S(2)}, u32[]{:S(2)}) collective-permute-start(f32[10,3,16,128]{3,2,1,0:T(8,128)} %get-tuple-element.58), channel_id=1, source_target_pairs={{64,0},{128,64},{192,128},{256,192},{320,256},{384,320},{448,384},... | collective-permute-start | bytes 737288 | tf_op jit(solution)/shard_map/ppermute | solution.py:40
  78.3 3.4 %collective-permute-start = (f32[10,3,16,128]{3,2,1,0:T(8,128)}, f32[10,3,16,128]{3,2,1,0:T(8,128)S(1)}, u32[]{:S(2)}, u32[]{:S(2)}) collective-permute-start(f32[10,3,16,128]{3,2,1,0:T(8,128)} %get-tuple-element.57), channel_id=1, source_target_pairs={{0,64},{64,128},{128,192},{192,256},{256,320},{320,384},{384,448},... | collective-permute-start | bytes 737288 | tf_op jit(solution)/shard_map/ppermute | solution.py:39
  81.7 1.9 %fusion.79 = (f32[10,16,16,3]{3,2,1,0:T(8,128)}, f32[10,16,16,3]{3,2,1,0:T(8,128)}) fusion(f32[10,16,16,128]{3,2,1,0:T(8,128)S(1)} %constant_dynamic-update-slice_fusion), kind=kLoop, calls=%fused_computation.183 | loop fusion | bytes 122880 | tf_op jit(solution)/shard_map/slice | solution.py:36
  83.6 3.1 %copy.29 = f32[10,16,16,3]{2,1,3,0:T(8,128)} copy(f32[10,16,16,3]{3,2,1,0:T(8,128)} %get-tuple-element.54) | data formatting | bytes 61440 | tf_op jit(solution)/shard_map/slice | solution.py:37
  86.7 2.8 %collective-permute-start.5 = (f32[10,16,16,3]{2,1,3,0:T(8,128)}, f32[10,16,16,3]{2,1,3,0:T(8,128)}, u32[]{:S(2)}, u32[]{:S(2)}) collective-permute-start(f32[10,16,16,3]{2,1,3,0:T(8,128)} %copy.29), channel_id=1, source_target_pairs={{1,0},{2,1},{3,2},{4,3},{5,4},{6,5},{7,6},{0,7},{9,8},{10,9},{11,1... | collective-permute-start | bytes 92168 | tf_op jit(solution)/shard_map/ppermute | solution.py:40
  90.4 1.9 %collective-permute-start.3 = (f32[10,16,3,128]{3,1,2,0:T(8,128)}, f32[10,16,3,128]{3,1,2,0:T(8,128)}, u32[]{:S(2)}, u32[]{:S(2)}) collective-permute-start(f32[10,16,3,128]{3,1,2,0:T(8,128)} %copy.25), channel_id=1, source_target_pairs={{8,0},{16,8},{24,16},{32,24},{40,32},{48,40},{56,48},{0,56},{9,1},... | collective-permute-start | bytes 737288 | tf_op jit(solution)/shard_map/ppermute | solution.py:40
  92.4 3.4 %collective-permute-start.2 = (f32[10,16,3,128]{3,1,2,0:T(8,128)S(1)}, f32[10,16,3,128]{3,1,2,0:T(8,128)}, u32[]{:S(2)}, u32[]{:S(2)}) collective-permute-start(f32[10,16,3,128]{3,1,2,0:T(8,128)S(1)} %copy.23), channel_id=1, source_target_pairs={{0,8},{8,16},{16,24},{24,32},{32,40},{40,48},{48,56},{56,0},{1,9},... | collective-permute-start | bytes 737288 | tf_op jit(solution)/shard_map/ppermute | solution.py:39
  95.9 3.1 %copy.27 = f32[10,16,16,3]{2,1,3,0:T(8,128)} copy(f32[10,16,16,3]{3,2,1,0:T(8,128)} %get-tuple-element.53) | data formatting | bytes 61440 | tf_op jit(solution)/shard_map/slice | solution.py:36
  99.0 4.2 %collective-permute-start.4 = (f32[10,16,16,3]{2,1,3,0:T(8,128)}, f32[10,16,16,3]{2,1,3,0:T(8,128)}, u32[]{:S(2)}, u32[]{:S(2)}) collective-permute-start(f32[10,16,16,3]{2,1,3,0:T(8,128)} %copy.27), channel_id=1, source_target_pairs={{0,1},{1,2},{2,3},{3,4},{4,5},{5,6},{6,7},{7,0},{8,9},{9,10},{10,1... | collective-permute-start | bytes 92168 | tf_op jit(solution)/shard_map/ppermute | solution.py:39
  103.9 3.0 %copy.30 = f32[10,16,16,3]{3,2,1,0:T(8,128)} copy(f32[10,16,16,3]{2,1,3,0:T(8,128)} %collective-permute-done.5) | data formatting | bytes 61440 | tf_op jit(solution)/shard_map/ppermute | solution.py:40
  106.9 3.1 %pad.24 = f32[10,22,22,3]{3,2,1,0:T(8,128)} pad(f32[10,16,16,3]{3,2,1,0:T(8,128)} %copy.30, f32[]{:T(128)} %constant.120.clone.1), padding=0_0x3_3x3_3x0_0 | pad | bytes 88804 | tf_op jit(solution)/shard_map/jit(_pad)/pad | solution.py:46
  110.0 3.0 %copy.28 = f32[10,16,16,3]{3,2,1,0:T(8,128)} copy(f32[10,16,16,3]{2,1,3,0:T(8,128)} %collective-permute-done.4) | data formatting | bytes 61440 | tf_op jit(solution)/shard_map/ppermute | solution.py:39
  113.0 1.7 %pad.23 = f32[10,22,22,3]{3,2,1,0:T(8,128)S(1)} pad(f32[10,16,16,3]{3,2,1,0:T(8,128)} %copy.28, f32[]{:T(128)} %constant.120.clone.1), padding=0_0x3_3x3_3x0_0 | pad | bytes 88804 | tf_op jit(solution)/shard_map/jit(_pad)/pad | solution.py:46
  114.8 1.1 copy.26
  122.4 1.1 fusion.57
  124.0 5.0 %fusion.13 = f32[6,16,16,128]{3,2,1,0:T(8,128)} fusion(f32[6,16,16,128]{3,2,1,0:T(8,128)S(1)} %copy-done.3, f32[10,16,16,128]{3,2,1,0:T(8,128)S(1)} %constant_dynamic-update-slice_fusion, f32[10,3,16,128]{3,2,1,0:T(8,128)S(1)} %collective-permute-done.1, f32[10,3,16,128]{3,2,1,0:T(8,128)S(1)} %collective-permute-done, f32[10,22,22,3]{3,2,1,0:T(8,128)S(1)} %copy-done, ...), kind=kLoop, calls=%fused_computation.38 | loop fusion | flops 15728640 | bytes 10458564 | tf_op jit(solution)/shard_map/add | solution.py:146
  (47 shorter events, 9.6 us)
Async XLA Ops:
  0.6 74.9 %copy-start.1 = (f32[4,16,16,128]{3,2,1,0:T(8,128)S(1)}, f32[4,16,16,128]{3,2,1,0:T(8,128)}, u32[]{:S(2)}) copy-start(f32[4,16,16,128]{3,2,1,0:T(8,128)} %param.12) | copy-start | bytes 1572868
  76.4 40.7 %collective-permute-start.1 = (f32[10,3,16,128]{3,2,1,0:T(8,128)}, f32[10,3,16,128]{3,2,1,0:T(8,128)S(1)}, u32[]{:S(2)}, u32[]{:S(2)}) collective-permute-start(f32[10,3,16,128]{3,2,1,0:T(8,128)} %get-tuple-element.58), channel_id=1, source_target_pairs={{64,0},{128,64},{192,128},{256,192},{320,256},{384,320},{448,384},... | collective-permute-start | bytes 737288 | tf_op jit(solution)/shard_map/ppermute | solution.py:40
  78.3 38.8 %collective-permute-start = (f32[10,3,16,128]{3,2,1,0:T(8,128)}, f32[10,3,16,128]{3,2,1,0:T(8,128)S(1)}, u32[]{:S(2)}, u32[]{:S(2)}) collective-permute-start(f32[10,3,16,128]{3,2,1,0:T(8,128)} %get-tuple-element.57), channel_id=1, source_target_pairs={{0,64},{64,128},{128,192},{192,256},{256,320},{320,384},{384,448},... | collective-permute-start | bytes 737288 | tf_op jit(solution)/shard_map/ppermute | solution.py:39
  86.7 12.3 %collective-permute-start.5 = (f32[10,16,16,3]{2,1,3,0:T(8,128)}, f32[10,16,16,3]{2,1,3,0:T(8,128)}, u32[]{:S(2)}, u32[]{:S(2)}) collective-permute-start(f32[10,16,16,3]{2,1,3,0:T(8,128)} %copy.29), channel_id=1, source_target_pairs={{1,0},{2,1},{3,2},{4,3},{5,4},{6,5},{7,6},{0,7},{9,8},{10,9},{11,1... | collective-permute-start | bytes 92168 | tf_op jit(solution)/shard_map/ppermute | solution.py:40
  90.4 24.3 %collective-permute-start.3 = (f32[10,16,3,128]{3,1,2,0:T(8,128)}, f32[10,16,3,128]{3,1,2,0:T(8,128)}, u32[]{:S(2)}, u32[]{:S(2)}) collective-permute-start(f32[10,16,3,128]{3,1,2,0:T(8,128)} %copy.25), channel_id=1, source_target_pairs={{8,0},{16,8},{24,16},{32,24},{40,32},{48,40},{56,48},{0,56},{9,1},... | collective-permute-start | bytes 737288 | tf_op jit(solution)/shard_map/ppermute | solution.py:40
  92.4 23.6 %collective-permute-start.2 = (f32[10,16,3,128]{3,1,2,0:T(8,128)S(1)}, f32[10,16,3,128]{3,1,2,0:T(8,128)}, u32[]{:S(2)}, u32[]{:S(2)}) collective-permute-start(f32[10,16,3,128]{3,1,2,0:T(8,128)S(1)} %copy.23), channel_id=1, source_target_pairs={{0,8},{8,16},{16,24},{24,32},{32,40},{40,48},{48,56},{56,0},{1,9},... | collective-permute-start | bytes 737288 | tf_op jit(solution)/shard_map/ppermute | solution.py:39
  99.0 11.0 %collective-permute-start.4 = (f32[10,16,16,3]{2,1,3,0:T(8,128)}, f32[10,16,16,3]{2,1,3,0:T(8,128)}, u32[]{:S(2)}, u32[]{:S(2)}) collective-permute-start(f32[10,16,16,3]{2,1,3,0:T(8,128)} %copy.27), channel_id=1, source_target_pairs={{0,1},{1,2},{2,3},{3,4},{4,5},{5,6},{6,7},{7,0},{8,9},{9,10},{10,1... | collective-permute-start | bytes 92168 | tf_op jit(solution)/shard_map/ppermute | solution.py:39
  113.0 4.1 %copy-start = (f32[10,22,22,3]{3,2,1,0:T(8,128)S(1)}, f32[10,22,22,3]{3,2,1,0:T(8,128)}, u32[]{:S(2)}) copy-start(f32[10,22,22,3]{3,2,1,0:T(8,128)} %pad.24) | copy-start | bytes 174244
  122.4 1.2 copy-start.2
  122.4 1.6 %copy-start.3 = (f32[6,16,16,128]{3,2,1,0:T(8,128)S(1)}, f32[6,16,16,128]{3,2,1,0:T(8,128)}, u32[]{:S(2)}) copy-start(f32[6,16,16,128]{3,2,1,0:T(8,128)} %param.11) | copy-start | bytes 2359300
where the time goes:
time: 130 us; the launch traced here: 129 us
  blocking collectives  68.3 us (53%)
  local copies, waits for them, and re-layouts  23.6 us (18%)
  starting transfers between devices  17.5 us (13%)
  other arithmetic  17.2 us (13%)
  between operations  2.32 us (2%)
    pmax x5, blocking collectives, over_axes(): value = lax.pmax(value, axis)  68.3 us
    ppermute x3, starting transfers between devices, padded_2(): lax.ppermute(last, axis, up)  10.9 us
    ppermute x3, starting transfers between devices, padded_2(): lax.ppermute(first, axis, [(b, a) for a, b in up])  6.62 us
    slice x5, local copies, waits for them, and re-layouts, padded_2(): last = lax.slice_in_dim(value, length - width, length, axis=dim)  6.03 us
    add x1, other arithmetic, body(): curvature_next = curvature + step * (eight_pi * stress - 0.5 * laplacian)  5.04 us
    ppermute x2, local copies, waits for them, and re-layouts, padded_2(): lax.ppermute(first, axis, [(b, a) for a, b in up])  4.07 us
    ppermute x2, local copies, waits for them, and re-layouts, padded_2(): lax.ppermute(last, axis, up)  4.07 us
    slice x2, local copies, waits for them, and re-layouts, padded_2(): first = lax.slice_in_dim(value, 0, width, axis=dim)  3.82 us
  transfers between devices with their start and end apart: 6, of which 0 were waited for; matrix products, arithmetic and copies ran while one was open for 17% of the time, Pallas kernels for 0%

commit v1 on v0

v1 whole, which is shorter than its diff:
```python
import math

import jax
import jax.numpy as jnp
from jax import lax
from jax.experimental import pallas as pl
from jax.experimental.pallas import tpu as pltpu
from jax.sharding import PartitionSpec as P

MESH = pl.DeviceIdType.MESH
MB = 16
second_stencil = (1.0 / 90.0, -3.0 / 20.0, 1.5, -49.0 / 18.0)
first_stencil = (-1.0 / 60.0, 3.0 / 20.0, -0.75)
sound_square = 0.25
sound_speed = 0.5
courant = 0.3
eight_pi = 8.0 * math.pi
pair_first = (0, 0, 0, 1, 1, 2)
pair_second = (0, 1, 2, 1, 2, 2)
diagonal = (0, 3, 5)

X, Y_LO, Y_HI, CORES = 4, 2, 4, 2
Y = Y_LO * Y_HI


def kernel(
    gx_size,
    metric_hbm, curvature_hbm, conserved_hbm, mask_hbm,
    plain, curv, rhs, held, slope, step_out,
    met, flu, inv, mask,
    pack_up, pack_down, from_low, from_high,
    own, got_1, got_2, got_3,
    local_sem, halo_send, halo_recv, max_send, max_recv,
):
    gx, gy, gz = lax.axis_index("gx"), lax.axis_index("gy"), lax.axis_index("gz")
    x, y_lo = lax.rem(gy, X), gy // X
    core, y_hi = lax.rem(gz, CORES), gz // CORES
    y = y_hi * Y_LO + y_lo
    gy_size, gz_size = X * Y_LO, Y_HI * CORES

    load_flu = pltpu.make_async_copy(conserved_hbm, flu.at[:, 1:17, 8:24, :], local_sem.at[0])
    load_mask = pltpu.make_async_copy(mask_hbm, mask, local_sem.at[1])
    load_met = pltpu.make_async_copy(metric_hbm, met.at[:, 3:19, 8:24, :], local_sem.at[2])
    load_curv = pltpu.make_async_copy(curvature_hbm, curv, local_sem.at[3])
    load_flu.start()
    load_mask.start()
    load_met.start()
    load_curv.start()
    load_plain = pltpu.make_async_copy(metric_hbm, plain, local_sem.at[4])
    load_plain.start()

    group_1 = []
    for dx in range(X):
        for dc in range(CORES):
            if dx or dc:
                group_1.append(
                    {"gx": gx, "gy": y_lo * X + lax.rem(x + dx, X), "gz": y_hi * CORES + lax.rem(core + dc, CORES)}
                )
    group_2 = []
    for dy in range(1, Y):
        there = lax.rem(y + dy, Y)
        group_2.append({"gx": gx, "gy": lax.rem(there, Y_LO) * X + x, "gz": (there // Y_LO) * CORES + core})
    group_3 = [{"gx": lax.rem(gx + dz, gx_size), "gy": gy, "gz": gz} for dz in range(1, gx_size)]
    x_up = {"gx": lax.rem(gx + 1, gx_size), "gy": gy, "gz": gz}
    x_down = {"gx": lax.rem(gx + gx_size - 1, gx_size), "gy": gy, "gz": gz}
    y_up = {"gx": gx, "gy": lax.rem(gy + 1, gy_size), "gz": gz}
    y_down = {"gx": gx, "gy": lax.rem(gy + gy_size - 1, gy_size), "gz": gz}
    z_up = {"gx": gx, "gy": gy, "gz": lax.rem(gz + 1, gz_size)}
    z_down = {"gx": gx, "gy": gy, "gz": lax.rem(gz + gz_size - 1, gz_size)}

    barrier = pltpu.get_barrier_semaphore()
    greeted = group_1 + group_2 + group_3 + [y_up, y_down, z_up, z_down]
    for peer in greeted:
        pl.semaphore_signal(barrier, inc=1, device_id=peer, device_id_type=MESH)

    load_flu.wait()
    load_mask.wait()
    lane = lax.broadcasted_iota(jnp.int32, (16, 128), 1)
    block = lane // MB
    matter = jnp.zeros((16, 128), jnp.int32)
    for b in range(128 // MB):
        matter = jnp.where(block == b, mask[0, 0, b], matter)
    live = matter > 0
    fastest = jnp.full((16, 128), sound_speed, jnp.float32)
    for i in range(16):
        density = flu[0, 1 + i, 8:24, :]
        largest = jnp.abs(flu[1, 1 + i, 8:24, :])
        for d in (2, 3):
            largest = jnp.maximum(largest, jnp.abs(flu[d, 1 + i, 8:24, :]))
        fastest = jnp.maximum(fastest, jnp.where(live, largest / density + sound_speed, sound_speed))
    own[0] = jnp.max(fastest, axis=0, keepdims=True)

    pl.semaphore_wait(barrier, len(greeted))

    sends = []

    def spread(stage, group, got, first):
        copies = []
        for slot, peer in enumerate(group):
            copy = pltpu.make_async_remote_copy(
                src_ref=own.at[stage],
                dst_ref=got.at[slot],
                send_sem=max_send.at[first + slot],
                recv_sem=max_recv.at[first + slot],
                device_id=peer,
                device_id_type=MESH,
            )
            copy.start()
            copies.append(copy)
        sends.extend(copies)
        return copies

    def gather(copies, stage, got):
        for copy in copies:
            copy.wait_recv()
        best = own[stage]
        for slot in range(len(copies)):
            best = jnp.maximum(best, got[slot])
        return best

    stage_1 = spread(0, group_1, got_1, 0)

    halos = []

    def send_halo(src, dst, peer):
        n = len(halos)
        copy = pltpu.make_async_remote_copy(
            src_ref=src,
            dst_ref=dst,
            send_sem=halo_send.at[n],
            recv_sem=halo_recv.at[n],
            device_id=peer,
            device_id_type=MESH,
        )
        copy.start()
        halos.append(copy)

    send_halo(flu.at[:, 16:17, 8:24, :], flu.at[:, 0:1, 8:24, :], x_up)
    send_halo(flu.at[:, 1:2, 8:24, :], flu.at[:, 17:18, 8:24, :], x_down)
    send_halo(flu.at[:, 1:17, 23:24, :], flu.at[:, 1:17, 7:8, :], y_up)
    send_halo(flu.at[:, 1:17, 8:9, :], flu.at[:, 1:17, 24:25, :], y_down)
    load_met.wait()
    send_halo(met.at[:, 16:19, 8:24, :], met.at[:, 0:3, 8:24, :], x_up)
    send_halo(met.at[:, 3:6, 8:24, :], met.at[:, 19:22, 8:24, :], x_down)
    send_halo(met.at[:, 3:19, 21:24, :], met.at[:, 3:19, 5:8, :], y_up)
    send_halo(met.at[:, 3:19, 8:11, :], met.at[:, 3:19, 24:27, :], y_down)

    group_of = lane // 4
    for f in range(5):
        up = jnp.zeros((16, 128), jnp.float32)
        down = jnp.zeros((16, 128), jnp.float32)
        for half in range(2):
            c = 2 * f + half
            for i in range(16):
                k = half * 16 + i
                plane = met[c, 3 + i, 8:24, :] if c < 6 else flu[c - 6, 1 + i, 8:24, :]
                up = jnp.where(group_of == k, pltpu.roll(plane, (4 * k + 4) % 128, 1), up)
                down = jnp.where(group_of == k, pltpu.roll(plane, 4 * k, 1) if k else plane, down)
        pack_up[f] = up
        pack_down[f] = down
    send_halo(pack_up, from_low, z_up)
    send_halo(pack_down, from_high, z_down)

    own[1] = gather(stage_1, 0, got_1)
    stage_2 = spread(1, group_2, got_2, len(group_1))
    own[2] = gather(stage_2, 1, got_2)
    stage_3 = spread(2, group_3, got_3, len(group_1) + len(group_2))

    for copy in halos:
        copy.wait_recv()
    load_curv.wait()
    load_plain.wait()

    for i in range(18):
        inv[i] = 1.0 / flu[0, i]

    def plane_step(i, carry):
        def z_halo(c):
            k = (c % 2) * 16 + i
            low = pltpu.roll(from_low[c // 2], lax.rem(124 - 4 * k + 128, 128), 1)
            high = pltpu.roll(from_high[c // 2], lax.rem(128 - 4 * k, 128), 1)
            return low, high

        def along_z(value, low, high, offset):
            if offset > 0:
                return pltpu.roll(jnp.where(lane < offset, high, value), 128 - offset, 1)
            return pltpu.roll(jnp.where(lane >= 128 + offset, low, value), -offset, 1)

        density = flu[0, 1 + i, 8:24, :]
        inverse = inv[1 + i, 8:24, :]
        moment = [flu[1 + d, 1 + i, 8:24, :] for d in range(3)]
        velocity = [m * inverse for m in moment]

        potential = {}
        for c in range(6):
            low, high = z_halo(c)
            value = met[c, 3 + i, 8:24, :]
            laplacian = (3.0 * second_stencil[3]) * value
            for n in range(3):
                o = 3 - n
                pairs = (
                    (met[c, 3 + i + o, 8:24, :], met[c, 3 + i - o, 8:24, :]),
                    (met[c, 3 + i, 8 + o : 24 + o, :], met[c, 3 + i, 8 - o : 24 - o, :]),
                    (along_z(value, low, high, o), along_z(value, low, high, -o)),
                )
                total = None
                for d, (above, below) in enumerate(pairs):
                    both = above + below
                    total = both if total is None else total + both
                    if c in diagonal:
                        change = above - below
                        key = (d, n)
                        potential[key] = change if key not in potential else potential[key] + change
                laplacian = laplacian + second_stencil[n] * total
            a, b = pair_first[c], pair_second[c]
            stress = moment[a] * velocity[b]
            if a == b:
                stress = stress + sound_square * density
            rhs[c, i] = eight_pi * stress - 0.5 * laplacian

        def cell(dim, offset):
            if dim == 0:
                state = [flu[c, 1 + i + offset, 8:24, :] for c in range(4)]
                inverse_there = inv[1 + i + offset, 8:24, :]
            elif dim == 1:
                state = [flu[c, 1 + i, 8 + offset : 24 + offset, :] for c in range(4)]
                inverse_there = inv[1 + i, 8 + offset : 24 + offset, :]
            else:
                state = []
                for c in range(4):
                    low, high = z_halo(6 + c)
                    here = density if c == 0 else moment[c - 1]
                    state.append(along_z(here, low, high, offset))
                inverse_there = 1.0 / state[0]
            speed_there = state[1 + dim] * inverse_there
            flux = [state[1 + dim]]
            for d in range(3):
                term = state[1 + d] * speed_there
                if d == dim:
                    term = term + sound_square * state[0]
                flux.append(term)
            return state, flux

        around = [None] * 4
        outflow = [None] * 4
        for dim in range(3):
            state_up, flux_up = cell(dim, 1)
            state_down, flux_down = cell(dim, -1)
            for c in range(4):
                both = state_up[c] + state_down[c]
                net = flux_up[c] - flux_down[c]
                around[c] = both if around[c] is None else around[c] + both
                outflow[c] = net if outflow[c] is None else outflow[c] + net
        here = [density] + moment
        for c in range(4):
            kept = here[c] + (0.5 * courant) * (around[c] - 6.0 * here[c])
            rate = -0.5 * outflow[c]
            if c > 0:
                gradient = None
                for n in range(3):
                    term = (-0.5 * first_stencil[n]) * potential[(c - 1, n)]
                    gradient = term if gradient is None else gradient + term
                rate = rate + density * gradient
            held[c, i] = jnp.where(live, kept, here[c])
            slope[c, i] = jnp.where(live, rate, 0.0)
        return carry

    lax.fori_loop(0, 16, plane_step, 0)

    best = gather(stage_3, 2, got_3)
    speed_max = jnp.max(best, axis=1, keepdims=True)
    step_out[...] = jnp.broadcast_to(courant / speed_max, (16, 128))

    for copy in halos + sends:
        copy.wait_send()


def advance(plain, curv, rhs, held, slope, step_in, metric_hbm, curvature_hbm, conserved_hbm, met, bent, flu, sem):
    step = step_in[...]
    copies = []

    def put(src, dst, at):
        copy = pltpu.make_async_copy(src.at[at], dst.at[at], sem.at[len(copies)])
        copy.start()
        copies.append(copy)

    for c in range(4):
        for i in range(16):
            flu[c, i] = held[c, i] + step * slope[c, i]
        put(flu, conserved_hbm, c)
    for c in range(6):
        for i in range(16):
            bend = curv[c, i]
            met[c, i] = plain[c, i] - (2.0 * step) * bend
            bent[c, i] = bend + step * rhs[c, i]
        put(met, metric_hbm, c)
        put(bent, curvature_hbm, c)
    for copy in copies:
        copy.wait()


def body(gx_size, metric, curvature, conserved, matter_mask):
    f32 = jnp.float32
    sym, fluid = metric.shape, conserved.shape
    n_max = (X * CORES - 1) + (Y - 1) + (gx_size - 1)
    anywhere = pl.BlockSpec(memory_space=pl.ANY)
    vmem = pl.BlockSpec(memory_space=pltpu.VMEM)
    in_hbm = lambda a: pltpu.with_memory_space_constraint(a, pltpu.HBM)
    in_vmem = lambda a: pltpu.with_memory_space_constraint(a, pltpu.VMEM)
    parts = pl.pallas_call(
        lambda *refs: kernel(gx_size, *refs),
        out_shape=tuple(pltpu.VMEM(s, f32) for s in (sym, sym, sym, fluid, fluid, (16, 128))),
        in_specs=[anywhere] * 4,
        out_specs=(vmem,) * 6,
        scratch_shapes=[
            pltpu.VMEM((6, 22, 32, 128), f32),
            pltpu.VMEM((4, 18, 32, 128), f32),
            pltpu.VMEM((18, 32, 128), f32),
            pltpu.SMEM(matter_mask.shape, jnp.int32),
            pltpu.VMEM((5, 16, 128), f32),
            pltpu.VMEM((5, 16, 128), f32),
            pltpu.VMEM((5, 16, 128), f32),
            pltpu.VMEM((5, 16, 128), f32),
            pltpu.VMEM((3, 1, 128), f32),
            pltpu.VMEM((X * CORES - 1, 1, 128), f32),
            pltpu.VMEM((Y - 1, 1, 128), f32),
            pltpu.VMEM((gx_size - 1, 1, 128), f32),
            pltpu.SemaphoreType.DMA((5,)),
            pltpu.SemaphoreType.DMA((10,)),
            pltpu.SemaphoreType.DMA((10,)),
            pltpu.SemaphoreType.DMA((n_max,)),
            pltpu.SemaphoreType.DMA((n_max,)),
        ],
        compiler_params=pltpu.CompilerParams(
            collective_id=0, has_side_effects=True, vmem_limit_bytes=24 * 1024 * 1024
        ),
        name="exchange",
    )(in_hbm(metric), in_hbm(curvature), in_hbm(conserved), in_hbm(matter_mask))
    return pl.pallas_call(
        advance,
        out_shape=tuple(jax.ShapeDtypeStruct(s, f32) for s in (sym, sym, fluid)),
        in_specs=[vmem] * 6,
        out_specs=(anywhere,) * 3,
        scratch_shapes=[
            pltpu.VMEM(sym, f32),
            pltpu.VMEM(sym, f32),
            pltpu.VMEM(fluid, f32),
            pltpu.SemaphoreType.DMA((16,)),
        ],
        compiler_params=pltpu.CompilerParams(vmem_limit_bytes=16 * 1024 * 1024),
        name="advance",
    )(*(in_vmem(a) for a in parts))


def solution(mesh):
    cells = P(None, "gx", "gy", "gz")
    return jax.shard_map(
        lambda *args: body(mesh.shape["gx"], *args),
        mesh=mesh,
        in_specs=(cells, cells, cells, P("gx", "gy", "gz")),
        out_specs=(cells, cells, cells),
        check_vma=False,
    )
```

time: 130 us -> 36 us (0.28)
  blocking collectives: 68.3 us -> 0 us
  Pallas kernels: 0 us -> 35.2 us
  local copies, waits for them, and re-layouts: 23.6 us -> 0 us
  starting transfers between devices: 17.5 us -> 0 us
  other arithmetic: 17.2 us -> 0 us
  between operations: 2.32 us -> 0.64 us
    pmax x5 -> x0, blocking collectives: 68.3 us -> none  [over_axes(): value = lax.pmax(value, axis)]
    pallas_call x0 -> x2, Pallas kernels: none -> 35.2 us  [the longest x1 33.8 us: body(): pl.pallas_call(lambda *refs: kernel(gx_size, *refs), out_shape=tuple((plt...]
    ppermute x6 -> x0, starting transfers between devices: 17.5 us -> none  [the longest x3 10.9 us: padded_2(): lax.ppermute(last, axis, up)]
    slice x7 -> x0, local copies, waits for them, and re-layouts: 9.84 us -> none  [the longest x5 6.03 us: padded_2(): last = lax.slice_in_dim(value, length - width, length, axis=dim)]
    ppermute x4 -> x0, local copies, waits for them, and re-layouts: 8.14 us -> none  [the longest x2 4.07 us: padded_2(): lax.ppermute(first, axis, [(b, a) for a, b in up])]
    add x2 -> x0, other arithmetic: 5.69 us -> none  [the longest x1 5.04 us: body(): curvature_next = curvature + step * (eight_pi * stress - 0.5 * laplacian)]
    pad x4 -> x0, local copies, waits for them, and re-layouts: 4.97 us -> none  [the longest x2 3.17 us: padded_2(): jnp.pad(high, around)]
    reduce_max x2 -> x0, other arithmetic: 2.65 us -> none  [the longest x1 1.55 us: body(): local_speed = jnp.max(jnp.where(cell_mask, speed, jnp.float32(sound_speed)))]
  transfers between devices with their start and end apart: 6 -> 0, of which waited for: 0 -> 0; matrix products, arithmetic and copies ran while one was open for 17% -> 0% of each run, Pallas kernels for 0% -> 0%
where the time goes in v1:
time: 36 us; the launch traced here: 35.9 us
  Pallas kernels  35.2 us (98%)
  between operations  0.64 us (2%)
    pallas_call x1, Pallas kernels, body(): pl.pallas_call(lambda *refs: kernel(gx_size, *refs), out_shape=tuple((plt...  33.8 us
    pallas_call x1, Pallas kernels, body(): pl.pallas_call(advance, out_shape=tuple((jax.ShapeDtypeStruct(s, f32) for...  1.46 us

profile of v1, /device:TPU:1, one launch (start us, length us, event | category | flops | bytes accessed | tf_op | source)
XLA Modules:
  0.0 35.9 jit_solution(9451292831444655286)
XLA Ops:
  0.6 33.8 %exchange.1 = (f32[6,16,16,128]{3,2,1,0:T(8,128)S(1)}, f32[6,16,16,128]{3,2,1,0:T(8,128)S(1)}, f32[6,16,16,128]{3,2,1,0:T(8,128)S(1)}, f32[4,16,16,128]{3,2,1,0:...) custom-call(f32[6,16,16,128]{3,2,1,0:T(8,128)} %refs_0_.1, f32[6,16,16,128]{3,2,1,0:T(8,128)} %refs_1_.1, ...), custom_call_target="tpu_custom_call" | custom-call | tf_op jit(solution)/shard_map/exchange/pallas_call | solution.py:310
  34.4 1.5 %advance.1 = (f32[6,16,16,128]{3,2,1,0:T(8,128)}, f32[6,16,16,128]{3,2,1,0:T(8,128)}, f32[4,16,16,128]{3,2,1,0:T(8,128)}) custom-call(f32[6,16,16,128]{3,2,1,0:T(8,128)S(1)} %get-tuple-element.9.plain, f32[6,16,16,128]{3,2,1,0:T(8,128)S(1)} %get-tuple-element.10.curv, f32[6,16,16,128]{3,2,1,0:T(8,128)S(1)} %get-tuple-element.11.rhs, ...), custom_call_target="tpu_custom_call" | custom-call | tf_op jit(solution)/shard_map/advance/pallas_call | solution.py:339

commit v2 on v1

--- a/solution.py
+++ b/solution.py
@@ -19,8 +19,14 @@
 pair_second = (0, 1, 2, 1, 2, 2)
 diagonal = (0, 3, 5)
 
+PITCH = 40
+
 X, Y_LO, Y_HI, CORES = 4, 2, 4, 2
 Y = Y_LO * Y_HI
+
+
+def far_first(n):
+    return sorted(range(n), key=lambda d: -min(d, n - d))
 
 
 def kernel(
@@ -30,7 +36,7 @@
     met, flu, inv, mask,
     pack_up, pack_down, from_low, from_high,
     own, got_1, got_2, got_3,
-    local_sem, halo_send, halo_recv, max_send, max_recv,
+    local_sem, halo_sem, max_send, max_recv, token_y, token_z,
 ):
     gx, gy, gz = lax.axis_index("gx"), lax.axis_index("gy"), lax.axis_index("gz")
     x, y_lo = lax.rem(gy, X), gy // X
@@ -44,23 +50,22 @@
     load_curv = pltpu.make_async_copy(curvature_hbm, curv, local_sem.at[3])
     load_flu.start()
     load_mask.start()
-    load_met.start()
-    load_curv.start()
     load_plain = pltpu.make_async_copy(metric_hbm, plain, local_sem.at[4])
-    load_plain.start()
 
     group_1 = []
-    for dx in range(X):
+    for dx in far_first(X):
         for dc in range(CORES):
             if dx or dc:
                 group_1.append(
                     {"gx": gx, "gy": y_lo * X + lax.rem(x + dx, X), "gz": y_hi * CORES + lax.rem(core + dc, CORES)}
                 )
     group_2 = []
-    for dy in range(1, Y):
+    for dy in far_first(Y)[:-1]:
         there = lax.rem(y + dy, Y)
         group_2.append({"gx": gx, "gy": lax.rem(there, Y_LO) * X + x, "gz": (there // Y_LO) * CORES + core})
-    group_3 = [{"gx": lax.rem(gx + dz, gx_size), "gy": gy, "gz": gz} for dz in range(1, gx_size)]
+    before = lax.rem(y + Y - 1, Y)
+    y_before = {"gx": gx, "gy": lax.rem(before, Y_LO) * X + x, "gz": (before // Y_LO) * CORES + core}
+    group_3 = [{"gx": lax.rem(gx + dz, gx_size), "gy": gy, "gz": gz} for dz in far_first(gx_size)[:-1]]
     x_up = {"gx": lax.rem(gx + 1, gx_size), "gy": gy, "gz": gz}
     x_down = {"gx": lax.rem(gx + gx_size - 1, gx_size), "gy": gy, "gz": gz}
     y_up = {"gx": gx, "gy": lax.rem(gy + 1, gy_size), "gz": gz}
@@ -68,13 +73,18 @@
     z_up = {"gx": gx, "gy": gy, "gz": lax.rem(gz + 1, gz_size)}
     z_down = {"gx": gx, "gy": gy, "gz": lax.rem(gz + gz_size - 1, gz_size)}
 
+    near_y = group_2[1:]
+    z_at = lambda d: {"gx": lax.rem(gx + gx_size + d, gx_size), "gy": gy, "gz": gz}
     barrier = pltpu.get_barrier_semaphore()
-    greeted = group_1 + group_2 + group_3 + [y_up, y_down, z_up, z_down]
+    greeted = group_1 + near_y + [z_at(1), z_at(-1), y_up, y_down, z_up, z_down]
     for peer in greeted:
         pl.semaphore_signal(barrier, inc=1, device_id=peer, device_id_type=MESH)
 
     load_flu.wait()
     load_mask.wait()
+    load_met.start()
+    load_plain.start()
+    load_curv.start()
     lane = lax.broadcasted_iota(jnp.int32, (16, 128), 1)
     block = lane // MB
     matter = jnp.zeros((16, 128), jnp.int32)
@@ -94,41 +104,48 @@
 
     sends = []
 
-    def spread(stage, group, got, first):
+    def spread(stage, group, got):
         copies = []
         for slot, peer in enumerate(group):
             copy = pltpu.make_async_remote_copy(
                 src_ref=own.at[stage],
                 dst_ref=got.at[slot],
-                send_sem=max_send.at[first + slot],
-                recv_sem=max_recv.at[first + slot],
+                send_sem=max_send,
+                recv_sem=max_recv.at[stage],
                 device_id=peer,
                 device_id_type=MESH,
             )
             copy.start()
             copies.append(copy)
         sends.extend(copies)
-        return copies
-
-    def gather(copies, stage, got):
-        for copy in copies:
-            copy.wait_recv()
+        return len(copies)
+
+    def arrive(ref, sem):
+        pltpu.make_async_copy(ref, ref, sem).wait()
+
+    def gather(count, stage, got):
+        arrive(got, max_recv.at[stage])
         best = own[stage]
-        for slot in range(len(copies)):
+        for slot in range(count):
             best = jnp.maximum(best, got[slot])
         return best
 
-    stage_1 = spread(0, group_1, got_1, 0)
+    def tell(token, peer):
+        pl.semaphore_signal(token, inc=1, device_id=peer, device_id_type=MESH)
+
+    stage_1 = spread(0, group_1, got_1)
+    tell(token_y, y_before)
+    for d in (1, -1):
+        tell(token_z.at[0], z_at(d))
 
     halos = []
 
     def send_halo(src, dst, peer):
-        n = len(halos)
         copy = pltpu.make_async_remote_copy(
             src_ref=src,
             dst_ref=dst,
-            send_sem=halo_send.at[n],
-            recv_sem=halo_recv.at[n],
+            send_sem=halo_sem.at[0],
+            recv_sem=halo_sem.at[1],
             device_id=peer,
             device_id_type=MESH,
         )
@@ -161,18 +178,25 @@
     send_halo(pack_up, from_low, z_up)
     send_halo(pack_down, from_high, z_down)
 
+    pl.semaphore_wait(token_z.at[0], 2)
+    for d in (2, -2):
+        tell(token_z.at[1], z_at(d))
+    pl.semaphore_wait(token_y, 1)
+
     own[1] = gather(stage_1, 0, got_1)
-    stage_2 = spread(1, group_2, got_2, len(group_1))
+    stage_2 = spread(1, group_2, got_2)
+    pl.semaphore_wait(token_z.at[1], 2)
+    for d in (2, -2):
+        tell(token_z.at[2], z_at(d))
     own[2] = gather(stage_2, 1, got_2)
-    stage_3 = spread(2, group_3, got_3, len(group_1) + len(group_2))
-
-    for copy in halos:
-        copy.wait_recv()
-    load_curv.wait()
-    load_plain.wait()
+    pl.semaphore_wait(token_z.at[2], 2)
+    stage_3 = spread(2, group_3, got_3)
+
+    all_halos = met.at[0:4, 0:14, 0:28, :]
+    arrive(all_halos, halo_sem.at[1])
 
     for i in range(18):
-        inv[i] = 1.0 / flu[0, i]
+        inv[i, 0:32, :] = 1.0 / flu[0, i, 0:32, :]
 
     def plane_step(i, carry):
         def z_halo(c):
@@ -267,12 +291,14 @@
 
     lax.fori_loop(0, 16, plane_step, 0)
 
+    load_curv.wait()
+    load_plain.wait()
     best = gather(stage_3, 2, got_3)
     speed_max = jnp.max(best, axis=1, keepdims=True)
     step_out[...] = jnp.broadcast_to(courant / speed_max, (16, 128))
 
-    for copy in halos + sends:
-        copy.wait_send()
+    arrive(all_halos, halo_sem.at[0])
+    arrive(met.at[0, 0:1, 0 : len(sends), :], max_send)
 
 
 def advance(plain, curv, rhs, held, slope, step_in, metric_hbm, curvature_hbm, conserved_hbm, met, bent, flu, sem):
@@ -302,7 +328,6 @@
 def body(gx_size, metric, curvature, conserved, matter_mask):
     f32 = jnp.float32
     sym, fluid = metric.shape, conserved.shape
-    n_max = (X * CORES - 1) + (Y - 1) + (gx_size - 1)
     anywhere = pl.BlockSpec(memory_space=pl.ANY)
     vmem = pl.BlockSpec(memory_space=pltpu.VMEM)
     in_hbm = lambda a: pltpu.with_memory_space_constraint(a, pltpu.HBM)
@@ -313,9 +338,9 @@
         in_specs=[anywhere] * 4,
         out_specs=(vmem,) * 6,
         scratch_shapes=[
-            pltpu.VMEM((6, 22, 32, 128), f32),
-            pltpu.VMEM((4, 18, 32, 128), f32),
-            pltpu.VMEM((18, 32, 128), f32),
+            pltpu.VMEM((6, 22, PITCH, 128), f32),
+            pltpu.VMEM((4, 18, PITCH, 128), f32),
+            pltpu.VMEM((18, PITCH, 128), f32),
             pltpu.SMEM(matter_mask.shape, jnp.int32),
             pltpu.VMEM((5, 16, 128), f32),
             pltpu.VMEM((5, 16, 128), f32),
@@ -326,10 +351,11 @@
             pltpu.VMEM((Y - 1, 1, 128), f32),
             pltpu.VMEM((gx_size - 1, 1, 128), f32),
             pltpu.SemaphoreType.DMA((5,)),
-            pltpu.SemaphoreType.DMA((10,)),
-            pltpu.SemaphoreType.DMA((10,)),
-            pltpu.SemaphoreType.DMA((n_max,)),
-            pltpu.SemaphoreType.DMA((n_max,)),
+            pltpu.SemaphoreType.DMA((2,)),
+            pltpu.SemaphoreType.DMA,
+            pltpu.SemaphoreType.DMA((3,)),
+            pltpu.SemaphoreType.REGULAR,
+            pltpu.SemaphoreType.REGULAR((3,)),
         ],
         compiler_params=pltpu.CompilerParams(
             collective_id=0, has_side_effects=True, vmem_limit_bytes=24 * 1024 * 1024

time: 36 us -> 33.1 us (0.919)
  Pallas kernels: 35.2 us -> 32.3 us
    pallas_call x1, Pallas kernels: 33.8 us -> 30.9 us  [body(): pl.pallas_call(lambda *refs: kernel(gx_size, *refs), out_shape=tuple((plt...]
where the time goes in v2:
time: 33.1 us; the launch traced here: 33 us
  Pallas kernels  32.3 us (98%)
  between operations  0.64 us (2%)
    pallas_call x1, Pallas kernels, body(): pl.pallas_call(lambda *refs: kernel(gx_size, *refs), out_shape=tuple((plt...  30.9 us
    pallas_call x1, Pallas kernels, body(): pl.pallas_call(advance, out_shape=tuple((jax.ShapeDtypeStruct(s, f32) for...  1.46 us

profile of v2, /device:TPU:1, one launch (start us, length us, event | category | flops | bytes accessed | tf_op | source)
XLA Modules:
  0.0 33.0 jit_solution(6021605600772840798)
XLA Ops:
  0.6 30.9 %exchange.1 = (f32[6,16,16,128]{3,2,1,0:T(8,128)S(1)}, f32[6,16,16,128]{3,2,1,0:T(8,128)S(1)}, f32[6,16,16,128]{3,2,1,0:T(8,128)S(1)}, f32[4,16,16,128]{3,2,1,0:...) custom-call(f32[6,16,16,128]{3,2,1,0:T(8,128)} %refs_0_.1, f32[6,16,16,128]{3,2,1,0:T(8,128)} %refs_1_.1, ...), custom_call_target="tpu_custom_call" | custom-call | tf_op jit(solution)/shard_map/exchange/pallas_call | solution.py:335
  31.5 1.5 %advance.1 = (f32[6,16,16,128]{3,2,1,0:T(8,128)}, f32[6,16,16,128]{3,2,1,0:T(8,128)}, f32[4,16,16,128]{3,2,1,0:T(8,128)}) custom-call(f32[6,16,16,128]{3,2,1,0:T(8,128)S(1)} %get-tuple-element.9.plain, f32[6,16,16,128]{3,2,1,0:T(8,128)S(1)} %get-tuple-element.10.curv, f32[6,16,16,128]{3,2,1,0:T(8,128)S(1)} %get-tuple-element.11.rhs, ...), custom_call_target="tpu_custom_call" | custom-call | tf_op jit(solution)/shard_map/advance/pallas_call | solution.py:365

commit v3 on v2

--- a/solution.py
+++ b/solution.py
@@ -20,6 +20,8 @@
 diagonal = (0, 3, 5)
 
 PITCH = 40
+
+EARLY = 3
 
 X, Y_LO, Y_HI, CORES = 4, 2, 4, 2
 Y = Y_LO * Y_HI
@@ -43,6 +45,7 @@
     core, y_hi = lax.rem(gz, CORES), gz // CORES
     y = y_hi * Y_LO + y_lo
     gy_size, gz_size = X * Y_LO, Y_HI * CORES
+    early = gx < EARLY
 
     load_flu = pltpu.make_async_copy(conserved_hbm, flu.at[:, 1:17, 8:24, :], local_sem.at[0])
     load_mask = pltpu.make_async_copy(mask_hbm, mask, local_sem.at[1])
@@ -102,10 +105,7 @@
 
     pl.semaphore_wait(barrier, len(greeted))
 
-    sends = []
-
     def spread(stage, group, got):
-        copies = []
         for slot, peer in enumerate(group):
             copy = pltpu.make_async_remote_copy(
                 src_ref=own.at[stage],
@@ -116,9 +116,6 @@
                 device_id_type=MESH,
             )
             copy.start()
-            copies.append(copy)
-        sends.extend(copies)
-        return len(copies)
 
     def arrive(ref, sem):
         pltpu.make_async_copy(ref, ref, sem).wait()
@@ -133,12 +130,10 @@
     def tell(token, peer):
         pl.semaphore_signal(token, inc=1, device_id=peer, device_id_type=MESH)
 
-    stage_1 = spread(0, group_1, got_1)
+    spread(0, group_1, got_1)
     tell(token_y, y_before)
     for d in (1, -1):
         tell(token_z.at[0], z_at(d))
-
-    halos = []
 
     def send_halo(src, dst, peer):
         copy = pltpu.make_async_remote_copy(
@@ -150,17 +145,19 @@
             device_id_type=MESH,
         )
         copy.start()
-        halos.append(copy)
-
+
+    def send_y():
+        send_halo(flu.at[:, 1:17, 23:24, :], flu.at[:, 1:17, 7:8, :], y_up)
+        send_halo(flu.at[:, 1:17, 8:9, :], flu.at[:, 1:17, 24:25, :], y_down)
+        send_halo(met.at[:, 3:19, 21:24, :], met.at[:, 3:19, 5:8, :], y_up)
+        send_halo(met.at[:, 3:19, 8:11, :], met.at[:, 3:19, 24:27, :], y_down)
+
+    load_met.wait()
+    pl.when(early)(send_y)
     send_halo(flu.at[:, 16:17, 8:24, :], flu.at[:, 0:1, 8:24, :], x_up)
     send_halo(flu.at[:, 1:2, 8:24, :], flu.at[:, 17:18, 8:24, :], x_down)
-    send_halo(flu.at[:, 1:17, 23:24, :], flu.at[:, 1:17, 7:8, :], y_up)
-    send_halo(flu.at[:, 1:17, 8:9, :], flu.at[:, 1:17, 24:25, :], y_down)
-    load_met.wait()
     send_halo(met.at[:, 16:19, 8:24, :], met.at[:, 0:3, 8:24, :], x_up)
     send_halo(met.at[:, 3:6, 8:24, :], met.at[:, 19:22, 8:24, :], x_down)
-    send_halo(met.at[:, 3:19, 21:24, :], met.at[:, 3:19, 5:8, :], y_up)
-    send_halo(met.at[:, 3:19, 8:11, :], met.at[:, 3:19, 24:27, :], y_down)
 
     group_of = lane // 4
     for f in range(5):
@@ -183,14 +180,19 @@
         tell(token_z.at[1], z_at(d))
     pl.semaphore_wait(token_y, 1)
 
-    own[1] = gather(stage_1, 0, got_1)
-    stage_2 = spread(1, group_2, got_2)
+    own[1] = gather(len(group_1), 0, got_1)
+    spread(1, group_2, got_2)
+    pl.when(jnp.logical_not(early))(send_y)
     pl.semaphore_wait(token_z.at[1], 2)
     for d in (2, -2):
         tell(token_z.at[2], z_at(d))
-    own[2] = gather(stage_2, 1, got_2)
-    pl.semaphore_wait(token_z.at[2], 2)
-    stage_3 = spread(2, group_3, got_3)
+
+    def pass_on():
+        own[2] = gather(len(group_2), 1, got_2)
+        pl.semaphore_wait(token_z.at[2], 2)
+        spread(2, group_3, got_3)
+
+    pl.when(jnp.logical_not(early))(pass_on)
 
     all_halos = met.at[0:4, 0:14, 0:28, :]
     arrive(all_halos, halo_sem.at[1])
@@ -290,15 +292,16 @@
         return carry
 
     lax.fori_loop(0, 16, plane_step, 0)
+    pl.when(early)(pass_on)
 
     load_curv.wait()
     load_plain.wait()
-    best = gather(stage_3, 2, got_3)
+    best = gather(len(group_3), 2, got_3)
     speed_max = jnp.max(best, axis=1, keepdims=True)
     step_out[...] = jnp.broadcast_to(courant / speed_max, (16, 128))
 
     arrive(all_halos, halo_sem.at[0])
-    arrive(met.at[0, 0:1, 0 : len(sends), :], max_send)
+    arrive(met.at[0, 0:1, 0 : len(group_1 + group_2 + group_3), :], max_send)
 
 
 def advance(plain, curv, rhs, held, slope, step_in, metric_hbm, curvature_hbm, conserved_hbm, met, bent, flu, sem):

time: 33.1 us -> 31.6 us (0.955)
  Pallas kernels: 32.3 us -> 30.8 us
    pallas_call x1, Pallas kernels: 30.9 us -> 29.4 us  [body(): pl.pallas_call(lambda *refs: kernel(gx_size, *refs), out_shape=tuple((plt...]
where the time goes in v3:
time: 31.6 us; the launch traced here: 31.5 us
  Pallas kernels  30.8 us (97%)
  between operations  0.64 us (2%)
    pallas_call x1, Pallas kernels, body(): pl.pallas_call(lambda *refs: kernel(gx_size, *refs), out_shape=tuple((plt...  29.4 us
    pallas_call x1, Pallas kernels, body(): pl.pallas_call(advance, out_shape=tuple((jax.ShapeDtypeStruct(s, f32) for...  1.46 us

profile of v3, /device:TPU:1, one launch (start us, length us, event | category | flops | bytes accessed | tf_op | source)
XLA Modules:
  0.0 31.5 jit_solution(8888201322334982184)
XLA Ops:
  0.6 29.4 %exchange.1 = (f32[6,16,16,128]{3,2,1,0:T(8,128)S(1)}, f32[6,16,16,128]{3,2,1,0:T(8,128)S(1)}, f32[6,16,16,128]{3,2,1,0:T(8,128)S(1)}, f32[4,16,16,128]{3,2,1,0:...) custom-call(f32[6,16,16,128]{3,2,1,0:T(8,128)} %refs_0_.1, f32[6,16,16,128]{3,2,1,0:T(8,128)} %refs_1_.1, ...), custom_call_target="tpu_custom_call" | custom-call | tf_op jit(solution)/shard_map/exchange/pallas_call | solution.py:338
  30.0 1.5 %advance.1 = (f32[6,16,16,128]{3,2,1,0:T(8,128)}, f32[6,16,16,128]{3,2,1,0:T(8,128)}, f32[4,16,16,128]{3,2,1,0:T(8,128)}) custom-call(f32[6,16,16,128]{3,2,1,0:T(8,128)S(1)} %get-tuple-element.9.plain, f32[6,16,16,128]{3,2,1,0:T(8,128)S(1)} %get-tuple-element.10.curv, f32[6,16,16,128]{3,2,1,0:T(8,128)S(1)} %get-tuple-element.11.rhs, ...), custom_call_target="tpu_custom_call" | custom-call | tf_op jit(solution)/shard_map/advance/pallas_call | solution.py:368
